TPU v7x, 32 devices: a whole 2x2x4 slice. The times are simulated.
32 devices in a mesh: groups: 2 (over y), px: 16 (over z, x, core).
Axes of the slice: x: 2, y: 2, z: 4, core: 2. Of those that a mesh axis runs over, the one named last changes fastest.
Arguments:
- features: bfloat16 [32, 256, 256, 256], P(None, ('groups', 'px')), parts along dimension 1, may hold values from -6 to 6
- pointwise_weight: bfloat16 [32, 32], replicated, may hold values from -1 to 1
- pointwise_bias: float32 [32], replicated, may hold values from -3 to 3
- spectral_weight: float32 [2, 32, 32, 16384], P(None, None, None, 'px'), may hold values from -6 to 6
Outputs:
- updated: bfloat16 [32, 256, 256, 256], P(None, ('groups', 'px')), parts along dimension 1
There are 2 independent parts, one for each index of `groups`. A program takes and returns all parts, laid end to end along the dimension named above; an argument that names none is the same for every part. Nothing has to cross between parts.
All inputs are finite; a program needn't handle non-finite values.
Results may differ from a plain program's by a relative error of at most 0.0025.
Values sent between devices are 32-bit elements; how exact they have to be, the bound alone decides.
A program may use at most 256 MiB of HBM per device.

v0:
```python
import functools
import math

import jax
import jax.numpy as jnp
import numpy as np
from jax import lax
from jax.experimental import pallas as pl
from jax.experimental.pallas import tpu as pltpu
from jax.sharding import PartitionSpec as P

KX = 32
KY = 32
KZ = 16
LANES = 128
PACK = LANES // KZ
ROWS = 16

TWO_PI = 2.0 * math.pi


def signed_modes(number):
    ladder = np.arange(number)
    return np.where(ladder < number // 2, ladder, ladder - number)


def phase_table(length, frequency):
    product = np.arange(length)[:, None] * frequency[None, :] % length
    return product.astype(np.float32) * np.float32(TWO_PI / length)


def rounded(table):
    return np.asarray(table).astype(jnp.bfloat16)


def split(table):
    high = rounded(table)
    return high, rounded(table - high.astype(np.float32))


def forward_table(length):
    phase = phase_table(length, signed_modes(KX))
    cosine, sine = np.cos(phase), np.sin(phase)
    return np.stack([np.stack([cosine, -sine], axis=1), np.stack([sine, cosine], axis=1)], axis=0)


def inverse_table(length):
    phase = phase_table(length, signed_modes(KX))
    cosine, sine = np.cos(phase), np.sin(phase)
    return np.stack([np.stack([cosine, sine], axis=1), np.stack([-sine, cosine], axis=1)], axis=0)


def packed_z_table(depth):
    phase = phase_table(depth, np.arange(KZ))
    table = np.zeros((PACK, depth, 2, PACK, KZ), np.float32)
    for c in range(PACK):
        table[c, :, 0, c] = np.cos(phase)
        table[c, :, 1, c] = -np.sin(phase)
    return rounded(table.reshape(PACK * depth, 2 * LANES))


def forward_kernel(f_ref, z_ref, y_ref, out_ref):
    groups = f_ref.shape[0] // PACK
    for g in range(groups):
        wide = jnp.concatenate([f_ref[g * PACK + c, 0] for c in range(PACK)], axis=1)
        along = jnp.dot(wide, z_ref[...], preferred_element_type=jnp.float32)
        high = along.astype(jnp.bfloat16)
        low = (along - high.astype(jnp.float32)).astype(jnp.bfloat16)
        both = jnp.dot(y_ref[...], high, preferred_element_type=jnp.float32)
        rest = jnp.dot(y_ref[: 2 * KY], low, preferred_element_type=jnp.float32)
        total = both[: 2 * KY] + both[2 * KY :] + rest
        cosine, sine = total[:KY], total[KY:]
        out_ref[:, 0, g, :] = cosine[:, :LANES] + sine[:, LANES:]
        out_ref[:, 0, groups + g, :] = cosine[:, LANES:] - sine[:, :LANES]


def spectra_local(features):
    channels, planes, height, depth = features.shape
    groups = channels // PACK
    y_phase = phase_table(height, signed_modes(KY)).T
    high, low = split(np.concatenate([np.cos(y_phase), np.sin(y_phase)], axis=0))
    return pl.pallas_call(
        forward_kernel,
        grid=(planes,),
        out_shape=jax.ShapeDtypeStruct((KY, planes, 2 * groups, LANES), jnp.float32),
        in_specs=[
            pl.BlockSpec((channels, 1, height, depth), lambda x: (0, x, 0, 0)),
            pl.BlockSpec((PACK * depth, 2 * LANES), lambda x: (0, 0)),
            pl.BlockSpec((4 * KY, height), lambda x: (0, 0)),
        ],
        out_specs=pl.BlockSpec((KY, 1, 2 * groups, LANES), lambda x: (0, x, 0, 0)),
        compiler_params=pltpu.CompilerParams(vmem_limit_bytes=48 << 20),
        name="forward_planes",
    )(features, jnp.asarray(packed_z_table(depth)), jnp.asarray(np.concatenate([high, low], axis=0)))


def contract(left, right):
    return jnp.einsum("im,iom->om", left, right, precision=lax.Precision.HIGHEST)


def mix_modes(spectrum, weights):
    real_part = contract(spectrum[0], weights[0]) - contract(spectrum[1], weights[1])
    imag_part = contract(spectrum[0], weights[1]) + contract(spectrum[1], weights[0])
    return jnp.stack([real_part, imag_part])


def inverse_kernel(f_ref, q_ref, place_ref, y_ref, z_ref, mix_ref, bias_ref, out_ref, held):
    channels, _, height, depth = f_ref.shape
    lane = lax.broadcasted_iota(jnp.int32, (height, LANES), 1)

    def along_y(c, carry):
        modes = q_ref[0, c]
        high = modes.astype(jnp.bfloat16)
        low = (modes - high.astype(jnp.float32)).astype(jnp.bfloat16)
        both = jnp.concatenate([high, low], axis=0)
        placed = jnp.dot(both, place_ref[...], preferred_element_type=jnp.float32)
        placed = placed.astype(jnp.bfloat16)
        high = jnp.concatenate([placed[:KY, :LANES], placed[:KY, LANES:]], axis=0)
        low = jnp.concatenate([placed[KY:, :LANES], placed[KY:, LANES:]], axis=0)
        stack = jnp.concatenate([high, high, low], axis=0)
        value = jnp.dot(y_ref[...], stack, preferred_element_type=jnp.float32)
        top = value.astype(jnp.bfloat16).astype(jnp.float32)
        part = jnp.where((lane >= 2 * KZ) & (lane < 4 * KZ), value - top, top)
        held[c] = jnp.where(lane < 6 * KZ, part, bias_ref[c]).astype(jnp.bfloat16)
        return carry

    lax.fori_loop(0, channels, along_y, 0, unroll=4)

    def finish(t, carry):
        rows = pl.ds(pl.multiple_of(t * ROWS, ROWS), ROWS)
        local = f_ref[:, 0, rows, :].reshape(channels * ROWS, depth)
        waves = held[:, rows, :].reshape(channels * ROWS, LANES)
        summed = jnp.dot(mix_ref[...], local, preferred_element_type=jnp.float32)
        summed = summed + jnp.dot(waves, z_ref[...], preferred_element_type=jnp.float32)
        inner = summed * (0.7978845608 + (0.7978845608 * 0.044715) * (summed * summed))
        half = 0.5 * summed
        result = (half + half * jnp.tanh(inner)).astype(jnp.bfloat16)
        out_ref[:, 0, rows, :] = result.reshape(channels, ROWS, depth)
        return carry

    lax.fori_loop(0, height // ROWS, finish, 0)


def finish_planes(modes, features, pointwise_weight, pointwise_bias, cells):
    channels, planes, height, depth = features.shape
    y_phase = phase_table(height, signed_modes(KY))
    high, low = split(np.concatenate([np.cos(y_phase), np.sin(y_phase)], axis=1))
    y_table = np.concatenate([high, low, high], axis=1)
    z_phase = phase_table(depth, np.arange(KZ)).T
    factor = (np.where(np.arange(KZ) == 0, 1.0, 2.0) / cells).astype(np.float32)[:, None]
    high, low = split(np.concatenate([factor * np.cos(z_phase), -factor * np.sin(z_phase)], axis=0))
    ones = np.zeros((2 * KZ, depth), np.float32)
    ones[:3] = 1.0
    z_table = np.concatenate([high, high, low, rounded(ones)], axis=0)
    mix = pointwise_weight[:, None, :, None] * jnp.eye(ROWS, dtype=jnp.bfloat16)[None, :, None, :]
    mix = mix.reshape(channels * ROWS, channels * ROWS)
    first = lax.reduce_precision(pointwise_bias, 8, 7)
    second = lax.reduce_precision(pointwise_bias - first, 8, 7)
    third = pointwise_bias - first - second
    bias = jnp.stack([first, second, third], axis=1)
    bias = jnp.pad(bias, ((0, 0), (6 * KZ, LANES - 6 * KZ - 3)))[:, None, :]
    same = np.eye(2 * KZ, dtype=np.float32)
    turned = np.roll(same, KZ, axis=1) * np.where(np.arange(2 * KZ) < KZ, -1.0, 1.0)
    repeats = LANES // (2 * KZ)
    place = np.concatenate([np.tile(same, (1, repeats)), np.tile(turned, (1, repeats))], axis=1)
    plane = pl.BlockSpec((channels, 1, height, depth), lambda x: (0, x, 0, 0))
    return pl.pallas_call(
        inverse_kernel,
        grid=(planes,),
        out_shape=jax.ShapeDtypeStruct(features.shape, jnp.bfloat16),
        in_specs=[
            plane,
            pl.BlockSpec((1, channels, KY, 2 * KZ), lambda x: (x, 0, 0, 0)),
            pl.BlockSpec((2 * KZ, 2 * LANES), lambda x: (0, 0)),
            pl.BlockSpec((height, 6 * KY), lambda x: (0, 0)),
            pl.BlockSpec((LANES, depth), lambda x: (0, 0)),
            pl.BlockSpec((channels * ROWS, channels * ROWS), lambda x: (0, 0)),
            pl.BlockSpec((channels, 1, LANES), lambda x: (0, 0, 0)),
        ],
        out_specs=plane,
        scratch_shapes=[pltpu.VMEM((channels, height, LANES), jnp.bfloat16)],
        compiler_params=pltpu.CompilerParams(vmem_limit_bytes=56 << 20),
        name="inverse_planes",
    )(features, modes, jnp.asarray(rounded(place)), jnp.asarray(y_table), jnp.asarray(z_table), mix, bias)


def on_device(parts, features, pointwise_weight, pointwise_bias, spectral_weight):
    channels, planes, height, depth = features.shape
    groups = channels // PACK
    length = planes * parts
    held_y = max(KY // parts, 1)
    cuts = parts * held_y // KY
    held_z = KZ // cuts
    exact = functools.partial(jnp.einsum, precision=lax.Precision.HIGHEST)

    sent = spectra_local(features)
    if cuts > 1:
        sent = sent.reshape(KY, planes, 2 * channels, cuts, held_z).transpose(0, 3, 1, 2, 4)
    sent = sent.reshape(parts, held_y * planes * 2 * channels * held_z // LANES, LANES)
    gathered = lax.all_to_all(sent, "px", split_axis=0, concat_axis=0, tiled=True)
    gathered = gathered.reshape(parts, held_y, planes, 2, channels, held_z)
    table = jnp.asarray(forward_table(length).reshape(2, parts, planes, 2, KX))
    spectrum = exact("sjprck,rsptm->tcjkm", gathered, table)
    blended = mix_modes(spectrum.reshape(2, channels, held_y * held_z * KX), spectral_weight)
    blended = blended.reshape(2, channels, held_y, held_z, KX)
    table = jnp.asarray(inverse_table(length).reshape(2, parts, planes, 2, KX))
    sent = exact("rcjkm,rsptm->spjtck", blended, table)
    sent = sent.reshape(parts, held_y * planes * 2 * channels * held_z // LANES, LANES)
    spread = lax.all_to_all(sent, "px", split_axis=0, concat_axis=0, tiled=True)
    spread = spread.reshape(KY // held_y, cuts, planes, held_y, 2, channels, held_z)
    modes = spread.transpose(2, 5, 0, 3, 4, 1, 6).reshape(planes, channels, KY, 2 * KZ)
    return finish_planes(
        modes, features, pointwise_weight, pointwise_bias, 1.0 * length * height * depth
    )


def solution(mesh):
    in_specs = (P(None, ("groups", "px"), None, None), P(), P(), P(None, None, None, "px"))
    out_specs = P(None, ("groups", "px"), None, None)
    return jax.shard_map(
        functools.partial(on_device, mesh.shape["px"]),
        mesh=mesh,
        in_specs=in_specs,
        out_specs=out_specs,
        check_vma=False,
    )
```

profile of v0, /device:TPU:9, one launch (start us, length us, event | category | flops | bytes accessed | tf_op | source)
XLA Modules:
  0.0 246.6 jit_solution(682119614319883899)
XLA Ops:
  0.0 1.2 copy-done
  1.2 0.8 copy-done.1
  2.1 27.0 %forward_planes.1 = f32[32,8,8,128]{3,2,1,0:T(8,128)S(1)} custom-call(bf16[32,8,256,256]{3,2,1,0:T(8,128)(2,1)} %f_ref.3, bf16[2048,256]{1,0:T(8,128)(2,1)S(1)} %copy-done, bf16[128,256]{1,0:T(8,128)(2,1)S(1)} %copy-done.1), custom_call_target="tpu_custom_call" | custom-call | tf_op jit(solution)/shard_map/forward_planes/pallas_call | solution.py:82
  29.1 31.7 %all_to_all.10 = f32[16,128,128]{2,1,0:T(8,128)S(1)} all-to-all(f32[16,128,128]{2,1,0:T(8,128)S(1)} %bitcast.74), channel_id=1, replica_groups=mesh['groups'=2,'px'=16] {'px'}, dimensions={0} | all-to-all | bytes 2097152 | tf_op jit(solution)/shard_map/all_to_all | solution.py:200
  60.7 4.5 %reshape.39 = f32[16,2,8,2,32,16]{5,4,3,2,1,0:T(8,128)} reshape(f32[16,128,128]{2,1,0:T(8,128)S(1)} %all_to_all.10) | data formatting | bytes 2097152 | tf_op jit(solution)/shard_map/reshape | solution.py:201
  65.3 7.3 %copy.35 = f32[16,2,8,2,32,16,1]{4,0,3,2,6,5,1:T(8,128)} copy(f32[16,2,8,2,32,16,1]{5,4,3,2,1,0,6:T(8,128)} %bitcast.75) | data formatting | bytes 2097152 | tf_op jit(solution)/shard_map/reshape | solution.py:201
  72.5 9.0 %convolution_bitcast_fusion.1 = f32[2,32,2,16,32]{4,1,0,3,2:T(8,128)S(1)} fusion(f32[16,2,8,2,32,16,1]{4,0,3,2,6,5,1:T(8,128)} %copy.35, f32[2,16,8,2,32,1,1]{4,1,0,2,3,6,5:T(8,128)S(1)} %copy-done.3), kind=kOutput, calls=%fused_computation.10 | convolution fusion | flops 201326592 | bytes 1376256 | tf_op jit(solution)/shard_map/sjprck,rsptm->tcjkm/dot_general | solution.py:203
  81.7 0.3 copy.27
  82.2 0.3 copy.28
  82.8 4.2 %fusion = (f32[1024,32]{0,1:T(8,128)S(1)}, f32[1024,32]{0,1:T(8,128)S(1)}, f32[1024,32]{0,1:T(8,128)S(1)}, f32[1024,32]{0,1:T(8,128)S(1)}) fusion(f32[2,32,32,1024]{3,2,1,0:T(8,128)} %param.14, f32[1024,32]{0,1:T(8,128)S(1)} %bitcast.79, f32[1024,32]{0,1:T(8,128)S(1)} %bitcast.78), kind=kLoop, calls=%fused_computation.2 | loop fusion | flops 8257536 | bytes 9175040 | tf_op jit(solution)/shard_map/im,iom->om/dot_general | solution.py:98
  87.2 0.3 copy.30
  87.7 0.3 copy.29
  88.0 5.0 %convolution_bitcast_fusion = f32[16,8,2,2,32,16]{4,0,3,1,5,2:T(8,128)} fusion(f32[2,16,8,2,32,1,1]{4,1,0,3,2,6,5:T(8,128)S(1)} %copy-done.2, f32[1,32,2,16,32]{4,1,0,3,2:T(8,128)S(1)} %copy.30, f32[1,32,2,16,32]{4,1,0,3,2:T(8,128)S(1)} %copy.29), kind=kOutput, calls=%fused_computation.8 | convolution fusion | flops 201392128 | bytes 1376256 | tf_op jit(solution)/shard_map/rcjkm,rsptm->spjtck/dot_general | solution.py:207
  93.0 7.0 %copy.31 = f32[16,8,2,2,32,16]{5,4,3,2,1,0:T(8,128)} copy(f32[16,8,2,2,32,16]{4,0,3,1,5,2:T(8,128)} %convolution_bitcast_fusion) | data formatting | bytes 2097152 | tf_op jit(solution)/shard_map/rcjkm,rsptm->spjtck/transpose | solution.py:207
  100.0 6.7 %reshape.40 = f32[16,128,128]{2,1,0:T(8,128)} reshape(f32[16,8,2,2,32,16]{5,4,3,2,1,0:T(8,128)} %copy.31) | data formatting | bytes 2097152 | tf_op jit(solution)/shard_map/reshape | solution.py:208
  106.7 4.4 %all-to-all-start.1 = ((f32[16,128,128]{2,1,0:T(8,128)}), f32[16,128,128]{2,1,0:T(8,128)S(1)}, u32[]{:S(2)}, u32[]{:S(2)}) async-start(f32[16,128,128]{2,1,0:T(8,128)} %reshape.40), calls=%async_computation.1 | async-start | bytes 2097152 | tf_op jit(solution)/shard_map/all_to_all | solution.py:209
  111.2 2.4 broadcast_multiply_fusion
  113.5 8.4 %mul.20.mix_ref = bf16[512,512]{1,0:T(8,128)(2,1)} reshape(bf16[32,16,32,16]{3,2,1,0:T(8,128)(2,1)} %broadcast_multiply_fusion) | data formatting | bytes 1048576 | tf_op jit(solution)/shard_map/mul | solution.py:155
  121.9 0.7 pad.4
  122.6 13.3 %all-to-all-done.1 = f32[16,128,128]{2,1,0:T(8,128)S(1)} async-done(((f32[16,128,128]{2,1,0:T(8,128)}), f32[16,128,128]{2,1,0:T(8,128)S(1)}, u32[]{:S(2)}, u32[]{:S(2)}) %all-to-all-start.1) | async-done | bytes 1048608 | tf_op jit(solution)/shard_map/all_to_all | solution.py:209
  136.0 4.5 %reshape.41 = f32[16,1,8,2,2,32,16]{6,5,4,3,2,0,1:T(8,128)} reshape(f32[16,128,128]{2,1,0:T(8,128)S(1)} %all-to-all-done.1) | data formatting | bytes 2097152 | tf_op jit(solution)/shard_map/reshape | solution.py:210
  140.5 6.8 %copy.32 = f32[8,32,16,2,2,1,16]{1,6,4,3,2,0,5:T(8,128)} copy(f32[8,32,16,2,2,1,16]{6,1,4,3,0,2,5:T(8,128)} %bitcast.76) | data formatting | bytes 2097152 | tf_op jit(solution)/shard_map/transpose | solution.py:211
  147.3 6.4 %copy.34.q_ref = f32[8,32,32,32]{3,2,1,0:T(8,128)} copy(f32[8,32,32,32]{1,3,2,0:T(8,128)} %bitcast.77) | data formatting | bytes 2097152 | tf_op jit(solution)/shard_map/reshape | solution.py:211
  153.7 92.9 %inverse_planes.1 = bf16[32,8,256,256]{3,2,1,0:T(8,128)(2,1)} custom-call(bf16[32,8,256,256]{3,2,1,0:T(8,128)(2,1)} %f_ref.3, f32[8,32,32,32]{3,2,1,0:T(8,128)} %copy.34.q_ref, bf16[32,256]{1,0:T(8,128)(2,1)} %constant.21.clone.place_ref, bf16[256,192]{1,0:T(8,128)(2,1)} %constant.22.clone.y_ref, bf16[128,256]{1,0:T(8,128)(2,1)} %constant.23.clone.z_ref, ...), custom_call_target="tpu_custom_call" | custom-call | tf_op jit(solution)/shard_map/inverse_planes/pallas_call | solution.py:167
  (20 shorter events, 1.0 us)
Async XLA Ops:
  0.0 1.2 copy-start
  1.2 0.8 copy-start.1
  65.3 7.3 %copy-start.3 = (f32[2,16,8,2,32,1,1]{4,1,0,2,3,6,5:T(8,128)S(1)}, f32[2,16,8,2,32,1,1]{4,1,0,2,3,6,5:T(8,128)}, u32[]{:S(2)}) copy-start(f32[2,16,8,2,32,1,1]{4,1,0,2,3,6,5:T(8,128)} %constant.31) | copy-start | bytes 196612
  87.0 1.0 copy-start.2
  100.0 11.0 %copy-start.5 = (f32[32]{0:T(128)S(1)}, f32[32]{0:T(128)}, u32[]{:S(2)}) copy-start(f32[32]{0:T(128)} %param.13) | copy-start | bytes 388
  100.0 11.1 %copy-start.4 = (bf16[32,32]{1,0:T(8,128)(2,1)S(1)}, bf16[32,32]{1,0:T(8,128)(2,1)}, u32[]{:S(2)}) copy-start(bf16[32,32]{1,0:T(8,128)(2,1)} %param.12) | copy-start | bytes 6148
  106.7 29.3 %all-to-all-start.1 = ((f32[16,128,128]{2,1,0:T(8,128)}), f32[16,128,128]{2,1,0:T(8,128)S(1)}, u32[]{:S(2)}, u32[]{:S(2)}) async-start(f32[16,128,128]{2,1,0:T(8,128)} %reshape.40), calls=%async_computation.1 | async-start | bytes 2097152 | tf_op jit(solution)/shard_map/all_to_all | solution.py:209
where the time goes:
time: 247 us
  Pallas kernels  120 us (49%)
  local copies, waits for them, and re-layouts  56.6 us (23%)
  blocking collectives  31.7 us (13%)
  matrix products  14 us (6%)
  waiting for transfers between devices  13.3 us (5%)
  other arithmetic  6.6 us (3%)
  starting transfers between devices  4.36 us (2%)
    pallas_call x1, Pallas kernels, finish_planes(): pl.pallas_call(inverse_kernel, grid=(planes,), out_shape=jax.ShapeDtypeSt...  92.9 us
    all_to_all x1, blocking collectives, on_device(): lax.all_to_all(sent, 'px', split_axis=0, concat_axis=0, tiled=True)  31.7 us
    pallas_call x1, Pallas kernels, spectra_local(): pl.pallas_call(forward_kernel, grid=(planes,), out_shape=jax.ShapeDtypeSt...  27 us
    all_to_all x1, waiting for transfers between devices, on_device(): spread = lax.all_to_all(sent, 'px', split_axis=0, concat_axis=0, tiled=True)  13.3 us
    reshape x2, local copies, waits for them, and re-layouts, on_device(): gathered = gathered.reshape(parts, held_y, planes, 2, channels, held_z)  11.8 us
    dot_general x1, matrix products, on_device(): spectrum = exact('sjprck,rsptm->tcjkm', gathered, table)  9.02 us
    mul x1, local copies, waits for them, and re-layouts, finish_planes(): pointwise_weight[:, None, :, None]  8.42 us
    transpose x1, local copies, waits for them, and re-layouts, on_device(): sent = exact('rcjkm,rsptm->spjtck', blended, table)  7.05 us
  transfers between devices with their start and end apart: 1, of which 1 were waited for; matrix products, arithmetic and copies ran while one was open for 5% of the time, Pallas kernels for 0%

commit v1 on v0

v1 whole, which is shorter than its diff:
```python
import functools
import math

import jax
import jax.numpy as jnp
import numpy as np
from jax import lax
from jax.experimental import pallas as pl
from jax.experimental.pallas import tpu as pltpu
from jax.sharding import PartitionSpec as P

KX = 32
KY = 32
KZ = 16
LANES = 128
PACK = LANES // KZ
QUAD = 4

TWO_PI = 2.0 * math.pi


def signed_modes(number):
    ladder = np.arange(number)
    return np.where(ladder < number // 2, ladder, ladder - number)


def phase_table(length, frequency):
    product = np.arange(length)[:, None] * frequency[None, :] % length
    return product.astype(np.float32) * np.float32(TWO_PI / length)


def rounded(table):
    return np.asarray(table).astype(jnp.bfloat16)


def split(table):
    high = rounded(table)
    return high, rounded(table - high.astype(np.float32))


def forward_table(length):
    phase = phase_table(length, signed_modes(KX))
    cosine, sine = np.cos(phase), np.sin(phase)
    return np.stack([np.stack([cosine, -sine], axis=1), np.stack([sine, cosine], axis=1)], axis=0)


def inverse_table(length):
    phase = phase_table(length, signed_modes(KX))
    cosine, sine = np.cos(phase), np.sin(phase)
    return np.stack([np.stack([cosine, sine], axis=1), np.stack([-sine, cosine], axis=1)], axis=0)


def halves(value):
    high = value.astype(jnp.bfloat16)
    return high, (value - high.astype(jnp.float32)).astype(jnp.bfloat16)


def product(left, right):
    return jnp.dot(left, right, preferred_element_type=jnp.float32)


def chosen(table, axis, width, count, which):
    place = lax.broadcasted_iota(jnp.int32, table.shape, axis) // width % count
    return jnp.where(place == which, table.astype(jnp.float32), 0.0).astype(jnp.bfloat16)


def whole(*shape):
    return pl.BlockSpec(shape, lambda *step: (0,) * len(shape))


def others(parts, act):
    me = lax.axis_index("px")

    def one(k, carry):
        act(lax.rem(me + k, parts))
        return carry

    lax.fori_loop(1, parts, one, 0)


def greet(parts):
    barrier = pltpu.get_barrier_semaphore()
    others(parts, lambda to: pl.semaphore_signal(barrier, inc=1, device_id={"px": to}))


def greeted(parts):
    pl.semaphore_wait(pltpu.get_barrier_semaphore(), parts - 1)


def share(parts, sent, out, at, sems):
    me = lax.axis_index("px")
    send, receive, local = sems

    def put(to):
        pltpu.make_async_remote_copy(
            src_ref=sent.at[to, at], dst_ref=out.at[me, at], send_sem=send, recv_sem=receive, device_id={"px": to}
        ).start()

    others(parts, put)
    pltpu.make_async_copy(sent.at[me, at], out.at[me, at], local).start()


def settle(parts, sent, out, sems):
    send, receive, local = sems
    pltpu.make_async_copy(sent.at[0], out.at[0], local).wait()
    most = pl.ds(0, parts - 1)
    every = pltpu.make_async_remote_copy(
        src_ref=sent.at[most], dst_ref=out.at[most], send_sem=send, recv_sem=receive,
        device_id={"px": lax.rem(lax.axis_index("px") + 1, parts)},
    )
    every.wait_send()
    every.wait_recv()


def spread_z(base_ref, z):
    depth = base_ref.shape[0]
    for c in range(PACK):
        z[c * depth : (c + 1) * depth] = chosen(base_ref[...], 1, KZ, PACK, c)


def plane_spectra(f_ref, z, y_ref, keep):
    groups = f_ref.shape[0] // PACK
    depth = f_ref.shape[3]
    for pair in range(0, groups, 2):
        along = [0.0, 0.0]
        for c in range(PACK):
            for n in range(2):
                along[n] += product(f_ref[(pair + n) * PACK + c, 0], z[c * depth : (c + 1) * depth])
        for n in range(2):
            g = pair + n
            high, low = halves(along[n])
            both = product(y_ref[...], high)
            rest = product(y_ref[: 2 * KY], low)
            total = both[: 2 * KY] + both[2 * KY :] + rest
            cosine, sine = total[:KY], total[KY:]
            keep(g, cosine[:, :LANES] + sine[:, LANES:])
            keep(groups + g, cosine[:, LANES:] - sine[:, :LANES])


def forward_kernel(f_ref, base_ref, y_ref, out_ref, z):
    @pl.when(pl.program_id(0) == 0)
    def start():
        spread_z(base_ref, z)

    def keep(row, value):
        out_ref[:, 0, row, :] = value

    plane_spectra(f_ref, z, y_ref, keep)


def forward_share_kernel(f_ref, base_ref, y_ref, out_ref, z, sent, send, receive, local):
    x = pl.program_id(0)
    parts, _, held_y = sent.shape[:3]

    @pl.when(x == 0)
    def start():
        greet(parts)
        spread_z(base_ref, z)

    def keep(row, value):
        sent[:, pl.ds(x, 1), :, row, :] = value.reshape(parts, 1, held_y, LANES)

    plane_spectra(f_ref, z, y_ref, keep)

    @pl.when(x == 0)
    def ready():
        greeted(parts)

    share(parts, sent, out_ref, x, (send, receive, local))

    @pl.when(x == pl.num_programs(0) - 1)
    def end():
        settle(parts, sent, out_ref, (send, receive, local))


def spectra(parts, features):
    channels, planes, height, depth = features.shape
    rows = 2 * channels // PACK
    y_phase = phase_table(height, signed_modes(KY)).T
    high, low = split(np.concatenate([np.cos(y_phase), np.sin(y_phase)], axis=0))
    z_phase = phase_table(depth, np.arange(KZ))
    base = rounded(np.concatenate([np.tile(np.cos(z_phase), (1, PACK)), np.tile(-np.sin(z_phase), (1, PACK))], axis=1))
    y_table = np.concatenate([high, low], axis=0)
    call = dict(
        grid=(planes,),
        in_specs=[
            pl.BlockSpec((channels, 1, height, depth), lambda x: (0, x, 0, 0)),
            whole(*base.shape),
            whole(*y_table.shape),
        ],
    )
    z = pltpu.VMEM((PACK * depth, 2 * LANES), jnp.bfloat16)
    if parts is None:
        kernel, shape = forward_kernel, (KY, planes, rows, LANES)
        call |= dict(
            out_specs=pl.BlockSpec((KY, 1, rows, LANES), lambda x: (0, x, 0, 0)),
            scratch_shapes=[z],
            compiler_params=pltpu.CompilerParams(vmem_limit_bytes=48 << 20),
            name="forward_planes",
        )
    else:
        kernel, shape = forward_share_kernel, (parts, planes, KY // parts, rows, LANES)
        call |= dict(
            out_specs=pl.BlockSpec(memory_space=pl.ANY),
            scratch_shapes=[z, pltpu.VMEM(shape, jnp.float32)] + [pltpu.SemaphoreType.DMA] * 3,
            compiler_params=pltpu.CompilerParams(vmem_limit_bytes=48 << 20, collective_id=0, has_side_effects=True),
            name="forward_share",
        )
    out_shape = jax.ShapeDtypeStruct(shape, jnp.float32)
    return pl.pallas_call(kernel, out_shape=out_shape, **call)(features, jnp.asarray(base), jnp.asarray(y_table))


def contract(left, right):
    return jnp.einsum("im,iom->om", left, right, precision=lax.Precision.HIGHEST)


def mix_modes(spectrum, weights):
    real_part = contract(spectrum[0], weights[0]) - contract(spectrum[1], weights[1])
    imag_part = contract(spectrum[0], weights[1]) + contract(spectrum[1], weights[0])
    return jnp.stack([real_part, imag_part])


def spectrum_table(length):
    table = np.broadcast_to(forward_table(length)[:, :, :, None, :], (2, length, 2, QUAD, KX))
    return split(table.reshape(2 * length, 2 * QUAD * KX))


def planes_table(length):
    table = inverse_table(length).transpose(0, 3, 2, 1)
    table = np.broadcast_to(table[:, None], (2, QUAD, KX, 2, length))
    return split(table.reshape(2 * QUAD * KX, 2 * length))


def modes_kernel(g_ref, fhigh_ref, flow_ref, ihigh_ref, ilow_ref, w_ref, out_ref, *scratch):
    fhigh, flow, ihigh, ilow, turned, spectrum, blended, placed, sent, send, receive, local = scratch
    parts, planes, held_y, rows, _ = g_ref.shape
    length = parts * planes
    channels = w_ref.shape[1]
    quads = KZ // QUAD
    groups = rows // 2
    here = pl.program_id(0)

    @pl.when(here == 0)
    def along_x():
        greet(parts)
        for q in range(QUAD):
            at = slice(q * 2 * length, (q + 1) * 2 * length)
            fhigh[at], flow[at] = chosen(fhigh_ref[...], 1, KX, QUAD, q), chosen(flow_ref[...], 1, KX, QUAD, q)
            ihigh[:, at], ilow[:, at] = chosen(ihigh_ref[...], 0, KX, QUAD, q), chosen(ilow_ref[...], 0, KX, QUAD, q)
        for j in range(held_y):
            for r in range(2):
                for g in range(groups):
                    tile = g_ref[:, :, j, r * groups + g, :].reshape(length, LANES)
                    turned[j, r, g * LANES : (g + 1) * LANES, :] = tile.T
        for b in range(held_y * quads):
            j, base = b // quads, b % quads * QUAD
            pieces = [turned[j, r, pl.ds(base + q, channels, stride=KZ), :] for q in range(QUAD) for r in range(2)]
            high, low = halves(jnp.concatenate(pieces, axis=1))
            spectrum[b] = product(high, fhigh[...]) + product(high, flow[...]) + product(low, fhigh[...])

    def mix(i, total):
        real, imag = total
        row = spectrum[here, pl.ds(i, 1), :]
        s_real, s_imag = row[:, :LANES], row[:, LANES:]
        w_real, w_imag = w_ref[0, i], w_ref[1, i]
        return real + (s_real * w_real - s_imag * w_imag), imag + (s_real * w_imag + s_imag * w_real)

    zero = jnp.zeros((channels, LANES), jnp.float32)
    real, imag = lax.fori_loop(0, channels, mix, (zero, zero), unroll=4)
    blended[here, :, :LANES] = real
    blended[here, :, LANES:] = imag

    for j in range(held_y):

        @pl.when(here == (j + 1) * quads - 1)
        def back_along_x():
            high, low = halves(blended[j * quads : (j + 1) * quads].reshape(quads * channels, 2 * LANES))
            value = product(high, ihigh[...]) + product(high, ilow[...]) + product(low, ihigh[...])
            for b in range(quads):
                for q in range(QUAD):
                    for r in range(2):
                        at = (q * 2 + r) * length
                        row = pl.ds(r * KZ + b * QUAD + q, channels, stride=2 * KZ)
                        placed[j, row, :] = value[b * channels : (b + 1) * channels, at : at + length]
            for h in range(sent.shape[3]):
                tile = placed[j, h * LANES : (h + 1) * LANES, :].T
                sent[:, j, :, h, :] = tile.reshape(parts, planes, LANES)
            if j == 0:
                greeted(parts)
            share(parts, sent, out_ref, j, (send, receive, local))
            if j == held_y - 1:
                settle(parts, sent, out_ref, (send, receive, local))


def mix_on_device(gathered, spectral_weight):
    parts, planes, held_y, rows, _ = gathered.shape
    length = parts * planes
    channels = spectral_weight.shape[1]
    blocks = held_y * KZ // QUAD
    tables = (*spectrum_table(length), *planes_table(length))
    packs = channels * 2 * KZ // LANES
    shape = (parts, held_y, planes, packs, LANES)
    wide = QUAD * 2 * length
    return pl.pallas_call(
        modes_kernel,
        grid=(blocks,),
        out_shape=jax.ShapeDtypeStruct(shape, jnp.float32),
        in_specs=[whole(*gathered.shape)]
        + [whole(*table.shape) for table in tables]
        + [pl.BlockSpec((2, channels, channels, LANES), lambda b: (0, 0, 0, b))],
        out_specs=pl.BlockSpec(memory_space=pl.ANY),
        scratch_shapes=[pltpu.VMEM((wide, 2 * LANES), jnp.bfloat16)] * 2
        + [pltpu.VMEM((2 * LANES, wide), jnp.bfloat16)] * 2
        + [
            pltpu.VMEM((held_y, 2, channels * KZ, length), jnp.float32),
            pltpu.VMEM((blocks, channels, 2 * LANES), jnp.float32),
            pltpu.VMEM((blocks, channels, 2 * LANES), jnp.float32),
            pltpu.VMEM((held_y, channels * 2 * KZ, length), jnp.float32),
            pltpu.VMEM(shape, jnp.float32),
        ]
        + [pltpu.SemaphoreType.DMA] * 3,
        compiler_params=pltpu.CompilerParams(vmem_limit_bytes=40 << 20, collective_id=1, has_side_effects=True),
        name="mix_share",
    )(gathered, *map(jnp.asarray, tables), spectral_weight)


def inverse_kernel(f_ref, q_ref, w_ref, left_ref, right_ref, zhigh_ref, zlow_ref, y_ref, bias_ref, out_ref, *scratch):
    mix, z, linear, other, waves = scratch
    channels, _, height, depth = f_ref.shape
    rows_each = height // channels
    packs = LANES // (2 * KZ)
    stacks = channels // packs
    step = pl.program_id(0)

    @pl.when(step == 0)
    def start():
        tall = product(left_ref[...], w_ref[...]).astype(jnp.bfloat16)
        wide = product(tall, right_ref[...])
        row = lax.broadcasted_iota(jnp.int32, wide.shape, 0)
        column = lax.broadcasted_iota(jnp.int32, wide.shape, 1)
        mix[...] = jnp.where(row % rows_each == column % rows_each, 0.5 * wide, 0.0).astype(jnp.bfloat16)
        z[...] = jnp.zeros_like(z)
        for k in range(packs):
            at = k * 2 * KZ
            z[k, at : at + 2 * KZ] = zhigh_ref[...]
            z[k, LANES + at : LANES + at + 2 * KZ] = zhigh_ref[...]
            z[k, 2 * LANES + at : 2 * LANES + at + 2 * KZ] = zlow_ref[...]

    def along_z():
        modes = jnp.concatenate([q_ref[:, :, 0, h, :].reshape(KY, LANES) for h in range(stacks)], axis=0)
        high, low = halves(modes)
        modes = jnp.concatenate([high, low, high], axis=1)
        first = lax.broadcasted_iota(jnp.int32, (KY, depth), 0) == 0
        for k in range(packs):
            value = product(modes, z[k])
            for h in range(stacks):
                c = h * packs + k
                part = value[h * KY : (h + 1) * KY]
                real = part[:, :depth] + jnp.where(first, 0.5 * bias_ref[c], 0.0)
                imag = part[:, depth:]
                waves[c, :KY], waves[c, 2 * KY : 3 * KY] = halves(real)
                waves[c, KY : 2 * KY], waves[c, 3 * KY :] = halves(imag)

    def pointwise(t, into):
        rows = pl.ds(pl.multiple_of(t * rows_each, rows_each), rows_each)
        local = f_ref[:, 0, rows, :].reshape(height, depth)
        into[:, rows, :] = product(mix[...], local).reshape(channels, rows_each, depth)

    def finish(c, held):
        wave = waves[c]
        stack = jnp.concatenate([wave, wave[: 2 * KY]], axis=0)
        half = product(y_ref[...], stack) + held[c]
        inner = half * (2.0 * 0.7978845608 + (8.0 * 0.7978845608 * 0.044715) * (half * half))
        out_ref[c, 0] = (half + half * jnp.tanh(inner)).astype(jnp.bfloat16)

    def work(into, held):
        along_z()

        def both(t, carry):
            pointwise(t, into)
            finish(t, held)
            return carry

        lax.fori_loop(0, channels, both, 0, unroll=8)

    @pl.when(step % 2 == 0)
    def even():
        work(linear, other)

    @pl.when(step % 2 == 1)
    def odd():
        work(other, linear)


def finish_planes(modes, features, pointwise_weight, pointwise_bias, cells):
    channels, planes, height, depth = features.shape
    owners, held_y, _, stacks, _ = modes.shape
    y_phase = phase_table(height, signed_modes(KY))
    high, low = split(np.concatenate([np.cos(y_phase), -np.sin(y_phase)], axis=1))
    y_table = np.concatenate([high, high, low], axis=1)
    z_phase = phase_table(depth, np.arange(KZ)).T
    factor = (0.5 * np.where(np.arange(KZ) == 0, 1.0, 2.0) / cells).astype(np.float32)[:, None]
    cosine, sine = factor * np.cos(z_phase), factor * np.sin(z_phase)
    z_high, z_low = split(np.block([[cosine, sine], [-sine, cosine]]))
    left = rounded(np.repeat(np.eye(channels, dtype=np.float32), height // channels, axis=0))
    plane = (channels, 1, height, depth)
    packs = LANES // (2 * KZ)
    return pl.pallas_call(
        inverse_kernel,
        grid=(planes + 1,),
        out_shape=jax.ShapeDtypeStruct(features.shape, jnp.bfloat16),
        in_specs=[
            pl.BlockSpec(plane, lambda x: (0, jnp.minimum(x, planes - 1), 0, 0)),
            pl.BlockSpec((owners, held_y, 1, stacks, LANES), lambda x: (0, 0, jnp.maximum(x - 1, 0), 0, 0)),
            whole(channels, channels),
            whole(height, channels),
            whole(channels, height),
            whole(*z_high.shape),
            whole(*z_low.shape),
            whole(*y_table.shape),
            pl.BlockSpec(memory_space=pltpu.SMEM),
        ],
        out_specs=pl.BlockSpec(plane, lambda x: (0, jnp.maximum(x - 1, 0), 0, 0)),
        scratch_shapes=[
            pltpu.VMEM((height, height), jnp.bfloat16),
            pltpu.VMEM((packs, 3 * LANES, 2 * depth), jnp.bfloat16),
            pltpu.VMEM((channels, height, depth), jnp.float32),
            pltpu.VMEM((channels, height, depth), jnp.float32),
            pltpu.VMEM((channels, 4 * KY, depth), jnp.bfloat16),
        ],
        compiler_params=pltpu.CompilerParams(vmem_limit_bytes=56 << 20),
        name="inverse_planes",
    )(
        features, modes, pointwise_weight, jnp.asarray(left), jnp.asarray(left.T), jnp.asarray(z_high),
        jnp.asarray(z_low), jnp.asarray(y_table), pointwise_bias,
    )


def by_einsum(parts, features, spectral_weight):
    channels, planes, height, depth = features.shape
    length = planes * parts
    held_y = max(KY // parts, 1)
    cuts = parts * held_y // KY
    held_z = KZ // cuts
    packs = LANES // (2 * KZ)
    exact = functools.partial(jnp.einsum, precision=lax.Precision.HIGHEST)
    exchange = functools.partial(lax.all_to_all, axis_name="px", split_axis=0, concat_axis=0, tiled=True)

    sent = spectra(None, features)
    sent = sent.reshape(KY, planes, 2 * channels, cuts, held_z).transpose(0, 3, 1, 2, 4)
    sent = sent.reshape(parts, held_y * planes * 2 * channels * held_z // LANES, LANES)
    gathered = exchange(sent).reshape(parts, held_y, planes, 2, channels, held_z)
    table = jnp.asarray(forward_table(length).reshape(2, parts, planes, 2, KX))
    spectrum = exact("sjprck,rsptm->tcjkm", gathered, table)
    blended = mix_modes(spectrum.reshape(2, channels, held_y * held_z * KX), spectral_weight)
    blended = blended.reshape(2, channels, held_y, held_z, KX)
    table = jnp.asarray(inverse_table(length).reshape(2, parts, planes, 2, KX))
    sent = exact("rcjkm,rsptm->spjtck", blended, table)
    sent = sent.reshape(parts, held_y * planes * 2 * channels * held_z // LANES, LANES)
    spread = exchange(sent).reshape(KY // held_y, cuts, planes, held_y, 2, channels // packs, packs, held_z)
    modes = spread.transpose(0, 3, 2, 5, 6, 4, 1, 7)
    return modes.reshape(KY // held_y, held_y, planes, channels // packs, LANES)


def on_device(parts, features, pointwise_weight, pointwise_bias, spectral_weight):
    channels, planes, height, depth = features.shape
    length = planes * parts
    if KY % parts == 0 and length == LANES:
        modes = mix_on_device(spectra(parts, features), spectral_weight)
    else:
        modes = by_einsum(parts, features, spectral_weight)
    return finish_planes(
        modes, features, pointwise_weight, pointwise_bias, 1.0 * length * height * depth
    )


def solution(mesh):
    in_specs = (P(None, ("groups", "px"), None, None), P(), P(), P(None, None, None, "px"))
    out_specs = P(None, ("groups", "px"), None, None)
    return jax.shard_map(
        functools.partial(on_device, mesh.shape["px"]),
        mesh=mesh,
        in_specs=in_specs,
        out_specs=out_specs,
        check_vma=False,
    )
```

time: 247 us -> 105 us (0.43)
  local copies, waits for them, and re-layouts: 56.6 us -> 3.48 us
  blocking collectives: 31.7 us -> 0 us
  Pallas kernels: 120 us -> 101 us
  matrix products: 14 us -> 0 us
  waiting for transfers between devices: 13.3 us -> 0 us
  other arithmetic: 6.6 us -> 0 us
  starting transfers between devices: 4.36 us -> 0 us
    all_to_all x1 -> x0, blocking collectives: 31.7 us -> none  [on_device(): lax.all_to_all(sent, 'px', split_axis=0, concat_axis=0, tiled=True)]
    reshape x5 -> x0, local copies, waits for them, and re-layouts: 29.3 us -> none  [the longest x2 11.8 us: on_device(): gathered = gathered.reshape(parts, held_y, planes, 2, channels, held_z)]
    pallas_call x2 -> x3, Pallas kernels: 120 us -> 101 us  [the longest x1 40.9 us: finish_planes(): pl.pallas_call(inverse_kernel, grid=(planes + 1,), out_shape=jax.ShapeDty...]
    dot_general x2 -> x0, matrix products: 14 us -> none  [the longest x1 9.02 us: on_device(): spectrum = exact('sjprck,rsptm->tcjkm', gathered, table)]
    transpose x2 -> x0, local copies, waits for them, and re-layouts: 13.9 us -> none  [the longest x1 7.05 us: on_device(): sent = exact('rcjkm,rsptm->spjtck', blended, table)]
    all_to_all x1 -> x0, waiting for transfers between devices: 13.3 us -> none  [on_device(): spread = lax.all_to_all(sent, 'px', split_axis=0, concat_axis=0, tiled=True)]
    mul x1 -> x0, local copies, waits for them, and re-layouts: 8.42 us -> none  [finish_planes(): pointwise_weight[:, None, :, None]]
    all_to_all x1 -> x0, starting transfers between devices: 4.36 us -> none  [on_device(): spread = lax.all_to_all(sent, 'px', split_axis=0, concat_axis=0, tiled=True)]
  transfers between devices with their start and end apart: 1 -> 0, of which waited for: 1 -> 0; matrix products, arithmetic and copies ran while one was open for 5% -> 0% of each run, Pallas kernels for 0% -> 0%
where the time goes in v1:
time: 105 us
  Pallas kernels  101 us (96%)
  local copies, waits for them, and re-layouts  3.48 us (3%)
    pallas_call x1, Pallas kernels, finish_planes(): pl.pallas_call(inverse_kernel, grid=(planes + 1,), out_shape=jax.ShapeDty...  40.9 us
    pallas_call x1, Pallas kernels, spectra(): pl.pallas_call(kernel, out_shape=out_shape, **call)  30.2 us
    pallas_call x1, Pallas kernels, mix_on_device(): pl.pallas_call(modes_kernel, grid=(blocks,), out_shape=jax.ShapeDtypeStru...  29.9 us
    unnamed x16, local copies, waits for them, and re-layouts  3.48 us

profile of v1, /device:TPU:9, one launch (start us, length us, event | category | flops | bytes accessed | tf_op | source)
XLA Modules:
  0.0 104.5 jit_solution(201878774034442015)
XLA Ops:
  0.0 0.0 copy-start.2
  0.0 0.0 copy-start.3
  0.0 0.0 copy-start.4
  0.0 0.0 copy-start.5
  0.0 0.0 copy-start
  0.0 0.0 copy-start.6
  0.0 1.0 copy-done.6
  1.1 0.0 copy-start.7
  1.1 1.4 %copy-done.7 = bf16[128,256]{1,0:T(8,128)(2,1)S(1)} copy-done((bf16[128,256]{1,0:T(8,128)(2,1)S(1)}, bf16[128,256]{1,0:T(8,128)(2,1)}, u32[]{:S(2)}) %copy-start.7) | copy-done | bytes 65560
  2.5 30.2 %forward_share.1.g_ref = f32[16,8,2,8,128]{4,3,2,1,0:T(8,128)S(1)} custom-call(bf16[32,8,256,256]{3,2,1,0:T(8,128)(2,1)} %f_ref.3, bf16[256,256]{1,0:T(8,128)(2,1)S(1)} %copy-done.6, bf16[128,256]{1,0:T(8,128)(2,1)S(1)} %copy-done.7), custom_call_target="tpu_custom_call" | custom-call | tf_op jit(solution)/shard_map/forward_share/pallas_call | solution.py:210
  32.7 0.0 copy-done.2
  32.7 0.0 copy-done.3
  32.7 0.0 copy-done.4
  32.8 0.0 copy-done.5
  32.8 0.0 copy-done
  32.8 29.9 %mix_share.1.q_ref = f32[16,2,8,8,128]{4,3,2,1,0:T(8,128)S(1)} custom-call(f32[16,8,2,8,128]{4,3,2,1,0:T(8,128)S(1)} %forward_share.1.g_ref, bf16[256,256]{1,0:T(8,128)(2,1)S(1)} %copy-done.5, bf16[256,256]{1,0:T(8,128)(2,1)S(1)} %copy-done.4, bf16[256,256]{1,0:T(8,128)(2,1)S(1)} %copy-done.3, bf16[256,256]{1,0:T(8,128)(2,1)S(1)} %copy-done.2, ...), custom_call_target="tpu_custom_call" | custom-call | tf_op jit(solution)/shard_map/mix_share/pallas_call | solution.py:304
  62.7 0.0 copy-start.1
  62.7 1.0 copy-done.1
  63.7 40.9 %inverse_planes.1 = bf16[32,8,256,256]{3,2,1,0:T(8,128)(2,1)} custom-call(bf16[32,8,256,256]{3,2,1,0:T(8,128)(2,1)} %f_ref.3, f32[16,2,8,8,128]{4,3,2,1,0:T(8,128)} %copy-done.1, bf16[32,32]{1,0:T(8,128)(2,1)} %w_ref.3, bf16[256,32]{1,0:T(8,128)(2,1)} %constant.28.clone.left_ref, bf16[32,256]{1,0:T(8,128)(2,1)} %constant.29.clone.right_ref, ...), custom_call_target="tpu_custom_call" | custom-call | tf_op jit(solution)/shard_map/inverse_planes/pallas_call | solution.py:408
Async XLA Ops:
  0.0 32.7 %copy-start.2 = (bf16[256,256]{1,0:T(8,128)(2,1)S(1)}, bf16[256,256]{1,0:T(8,128)(2,1)}, u32[]{:S(2)}) copy-start(bf16[256,256]{1,0:T(8,128)(2,1)} %constant.27.clone.ilow_ref) | copy-start | bytes 393220
  0.0 32.7 %copy-start.3 = (bf16[256,256]{1,0:T(8,128)(2,1)S(1)}, bf16[256,256]{1,0:T(8,128)(2,1)}, u32[]{:S(2)}) copy-start(bf16[256,256]{1,0:T(8,128)(2,1)} %constant.26.clone.ihigh_ref) | copy-start | bytes 393220
  0.0 32.7 %copy-start.4 = (bf16[256,256]{1,0:T(8,128)(2,1)S(1)}, bf16[256,256]{1,0:T(8,128)(2,1)}, u32[]{:S(2)}) copy-start(bf16[256,256]{1,0:T(8,128)(2,1)} %constant.25.clone.flow_ref) | copy-start | bytes 393220
  0.0 32.7 %copy-start.5 = (bf16[256,256]{1,0:T(8,128)(2,1)S(1)}, bf16[256,256]{1,0:T(8,128)(2,1)}, u32[]{:S(2)}) copy-start(bf16[256,256]{1,0:T(8,128)(2,1)} %constant.24.clone.fhigh_ref) | copy-start | bytes 393220
  0.0 32.7 %copy-start = (f32[2,32,32,1024]{3,2,1,0:T(8,128)S(1)}, f32[2,32,32,1024]{3,2,1,0:T(8,128)}, u32[]{:S(2)}) copy-start(f32[2,32,32,1024]{3,2,1,0:T(8,128)} %w_ref.2) | copy-start | bytes 25165828
  0.0 1.1 %copy-start.6 = (bf16[256,256]{1,0:T(8,128)(2,1)S(1)}, bf16[256,256]{1,0:T(8,128)(2,1)}, u32[]{:S(2)}) copy-start(bf16[256,256]{1,0:T(8,128)(2,1)} %constant.22.clone.base_ref) | copy-start | bytes 393220
  1.1 1.4 %copy-start.7 = (bf16[128,256]{1,0:T(8,128)(2,1)S(1)}, bf16[128,256]{1,0:T(8,128)(2,1)}, u32[]{:S(2)}) copy-start(bf16[128,256]{1,0:T(8,128)(2,1)} %constant.23.clone.y_ref) | copy-start | bytes 196612
  62.7 1.0 copy-start.1

commit v2 on v1

--- a/solution.py
+++ b/solution.py
@@ -15,6 +15,8 @@
 LANES = 128
 PACK = LANES // KZ
 QUAD = 4
+TOP = 8
+MOST = 63 << 20
 
 TWO_PI = 2.0 * math.pi
 
@@ -195,7 +197,7 @@
         call |= dict(
             out_specs=pl.BlockSpec((KY, 1, rows, LANES), lambda x: (0, x, 0, 0)),
             scratch_shapes=[z],
-            compiler_params=pltpu.CompilerParams(vmem_limit_bytes=48 << 20),
+            compiler_params=pltpu.CompilerParams(vmem_limit_bytes=MOST),
             name="forward_planes",
         )
     else:
@@ -203,7 +205,7 @@
         call |= dict(
             out_specs=pl.BlockSpec(memory_space=pl.ANY),
             scratch_shapes=[z, pltpu.VMEM(shape, jnp.float32)] + [pltpu.SemaphoreType.DMA] * 3,
-            compiler_params=pltpu.CompilerParams(vmem_limit_bytes=48 << 20, collective_id=0, has_side_effects=True),
+            compiler_params=pltpu.CompilerParams(vmem_limit_bytes=MOST, collective_id=0, has_side_effects=True),
             name="forward_share",
         )
     out_shape = jax.ShapeDtypeStruct(shape, jnp.float32)
@@ -241,22 +243,28 @@
     here = pl.program_id(0)
 
     @pl.when(here == 0)
-    def along_x():
+    def start():
         greet(parts)
         for q in range(QUAD):
             at = slice(q * 2 * length, (q + 1) * 2 * length)
             fhigh[at], flow[at] = chosen(fhigh_ref[...], 1, KX, QUAD, q), chosen(flow_ref[...], 1, KX, QUAD, q)
             ihigh[:, at], ilow[:, at] = chosen(ihigh_ref[...], 0, KX, QUAD, q), chosen(ilow_ref[...], 0, KX, QUAD, q)
-        for j in range(held_y):
+
+    for j in range(held_y):
+
+        @pl.when(here == j * quads)
+        def along_x(j=j):
             for r in range(2):
                 for g in range(groups):
                     tile = g_ref[:, :, j, r * groups + g, :].reshape(length, LANES)
-                    turned[j, r, g * LANES : (g + 1) * LANES, :] = tile.T
-        for b in range(held_y * quads):
-            j, base = b // quads, b % quads * QUAD
-            pieces = [turned[j, r, pl.ds(base + q, channels, stride=KZ), :] for q in range(QUAD) for r in range(2)]
-            high, low = halves(jnp.concatenate(pieces, axis=1))
-            spectrum[b] = product(high, fhigh[...]) + product(high, flow[...]) + product(low, fhigh[...])
+                    turned[r, g * LANES : (g + 1) * LANES, :] = tile.T
+            for b in range(quads):
+                pieces = [
+                    turned[r, pl.ds(b * QUAD + q, channels, stride=KZ), :] for q in range(QUAD) for r in range(2)
+                ]
+                high, low = halves(jnp.concatenate(pieces, axis=1))
+                value = product(high, fhigh[...]) + product(high, flow[...]) + product(low, fhigh[...])
+                spectrum[j * quads + b] = value
 
     def mix(i, total):
         real, imag = total
@@ -273,7 +281,7 @@
     for j in range(held_y):
 
         @pl.when(here == (j + 1) * quads - 1)
-        def back_along_x():
+        def back_along_x(j=j):
             high, low = halves(blended[j * quads : (j + 1) * quads].reshape(quads * channels, 2 * LANES))
             value = product(high, ihigh[...]) + product(high, ilow[...]) + product(low, ihigh[...])
             for b in range(quads):
@@ -312,14 +320,14 @@
         scratch_shapes=[pltpu.VMEM((wide, 2 * LANES), jnp.bfloat16)] * 2
         + [pltpu.VMEM((2 * LANES, wide), jnp.bfloat16)] * 2
         + [
-            pltpu.VMEM((held_y, 2, channels * KZ, length), jnp.float32),
+            pltpu.VMEM((2, channels * KZ, length), jnp.float32),
             pltpu.VMEM((blocks, channels, 2 * LANES), jnp.float32),
             pltpu.VMEM((blocks, channels, 2 * LANES), jnp.float32),
             pltpu.VMEM((held_y, channels * 2 * KZ, length), jnp.float32),
             pltpu.VMEM(shape, jnp.float32),
         ]
         + [pltpu.SemaphoreType.DMA] * 3,
-        compiler_params=pltpu.CompilerParams(vmem_limit_bytes=40 << 20, collective_id=1, has_side_effects=True),
+        compiler_params=pltpu.CompilerParams(vmem_limit_bytes=MOST, collective_id=1, has_side_effects=True),
         name="mix_share",
     )(gathered, *map(jnp.asarray, tables), spectral_weight)
 
@@ -339,30 +347,32 @@
         row = lax.broadcasted_iota(jnp.int32, wide.shape, 0)
         column = lax.broadcasted_iota(jnp.int32, wide.shape, 1)
         mix[...] = jnp.where(row % rows_each == column % rows_each, 0.5 * wide, 0.0).astype(jnp.bfloat16)
-        z[...] = jnp.zeros_like(z)
-        for k in range(packs):
-            at = k * 2 * KZ
-            z[k, at : at + 2 * KZ] = zhigh_ref[...]
-            z[k, LANES + at : LANES + at + 2 * KZ] = zhigh_ref[...]
-            z[k, 2 * LANES + at : 2 * LANES + at + 2 * KZ] = zlow_ref[...]
+        z[: 2 * KZ] = zhigh_ref[...]
+        z[2 * KZ : 4 * KZ] = zhigh_ref[...]
+        z[4 * KZ : 6 * KZ] = zlow_ref[...]
+        z[6 * KZ :] = jnp.zeros((LANES - 6 * KZ, 2 * depth), jnp.bfloat16)
 
     def along_z():
         modes = jnp.concatenate([q_ref[:, :, 0, h, :].reshape(KY, LANES) for h in range(stacks)], axis=0)
-        high, low = halves(modes)
-        modes = jnp.concatenate([high, low, high], axis=1)
-        first = lax.broadcasted_iota(jnp.int32, (KY, depth), 0) == 0
+        high = modes.astype(jnp.bfloat16).astype(jnp.float32)
+        low = modes - high
+        lane = lax.broadcasted_iota(jnp.int32, modes.shape, 1) // (2 * KZ)
+        first = lax.broadcasted_iota(jnp.int32, (TOP, depth), 0) == 0
         for k in range(packs):
-            value = product(modes, z[k])
+            turned = lambda value, to: pltpu.roll(value, (to - k) * 2 * KZ % LANES, 1)
+            left = jnp.where(lane == 0, turned(high, 0), jnp.where(lane == 1, turned(low, 1), turned(high, 2)))
+            value = product(jnp.where(lane < 3, left, 0.0).astype(jnp.bfloat16), z[...])
             for h in range(stacks):
                 c = h * packs + k
                 part = value[h * KY : (h + 1) * KY]
-                real = part[:, :depth] + jnp.where(first, 0.5 * bias_ref[c], 0.0)
+                top = part[:TOP, :depth] + jnp.where(first, 0.5 * bias_ref[c], 0.0)
+                real = jnp.concatenate([top, part[TOP:, :depth]], axis=0)
                 imag = part[:, depth:]
                 waves[c, :KY], waves[c, 2 * KY : 3 * KY] = halves(real)
                 waves[c, KY : 2 * KY], waves[c, 3 * KY :] = halves(imag)
 
     def pointwise(t, into):
-        rows = pl.ds(pl.multiple_of(t * rows_each, rows_each), rows_each)
+        rows = pl.ds(t * rows_each if isinstance(t, int) else pl.multiple_of(t * rows_each, rows_each), rows_each)
         local = f_ref[:, 0, rows, :].reshape(height, depth)
         into[:, rows, :] = product(mix[...], local).reshape(channels, rows_each, depth)
 
@@ -374,14 +384,22 @@
         out_ref[c, 0] = (half + half * jnp.tanh(inner)).astype(jnp.bfloat16)
 
     def work(into, held):
-        along_z()
-
-        def both(t, carry):
-            pointwise(t, into)
-            finish(t, held)
-            return carry
-
-        lax.fori_loop(0, channels, both, 0, unroll=8)
+        @pl.when(step == 0)
+        def first():
+            lax.fori_loop(0, channels, lambda t, carry: (pointwise(t, into), carry)[1], 0, unroll=8)
+
+        @pl.when(step == pl.num_programs(0) - 1)
+        def last():
+            along_z()
+            lax.fori_loop(0, channels, lambda t, carry: (finish(t, held), carry)[1], 0, unroll=8)
+
+        @pl.when((step > 0) & (step < pl.num_programs(0) - 1))
+        def middle():
+            along_z()
+
+            for t in range(channels):
+                pointwise(t, into)
+                finish(t, held)
 
     @pl.when(step % 2 == 0)
     def even():
@@ -404,7 +422,6 @@
     z_high, z_low = split(np.block([[cosine, sine], [-sine, cosine]]))
     left = rounded(np.repeat(np.eye(channels, dtype=np.float32), height // channels, axis=0))
     plane = (channels, 1, height, depth)
-    packs = LANES // (2 * KZ)
     return pl.pallas_call(
         inverse_kernel,
         grid=(planes + 1,),
@@ -423,12 +440,12 @@
         out_specs=pl.BlockSpec(plane, lambda x: (0, jnp.maximum(x - 1, 0), 0, 0)),
         scratch_shapes=[
             pltpu.VMEM((height, height), jnp.bfloat16),
-            pltpu.VMEM((packs, 3 * LANES, 2 * depth), jnp.bfloat16),
+            pltpu.VMEM((LANES, 2 * depth), jnp.bfloat16),
             pltpu.VMEM((channels, height, depth), jnp.float32),
             pltpu.VMEM((channels, height, depth), jnp.float32),
             pltpu.VMEM((channels, 4 * KY, depth), jnp.bfloat16),
         ],
-        compiler_params=pltpu.CompilerParams(vmem_limit_bytes=56 << 20),
+        compiler_params=pltpu.CompilerParams(vmem_limit_bytes=MOST),
         name="inverse_planes",
     )(
         features, modes, pointwise_weight, jnp.asarray(left), jnp.asarray(left.T), jnp.asarray(z_high),

time: 105 us -> 95.7 us (0.911)
  Pallas kernels: 101 us -> 95.2 us
  local copies, waits for them, and re-layouts: 3.48 us -> 0 us
    pallas_call x1, Pallas kernels: 40.9 us -> 34.3 us  [finish_planes(): pl.pallas_call(inverse_kernel, grid=(planes + 1,), out_shape=jax.ShapeDty...]
    unnamed x16 -> x0, local copies, waits for them, and re-layouts: 3.48 us -> none
where the time goes in v2:
time: 95.7 us; the launch traced here: 95.2 us
  Pallas kernels  95.2 us (99%)
    pallas_call x1, Pallas kernels, finish_planes(): pl.pallas_call(inverse_kernel, grid=(planes + 1,), out_shape=jax.ShapeDty...  34.3 us
    pallas_call x1, Pallas kernels, mix_on_device(): pl.pallas_call(modes_kernel, grid=(blocks,), out_shape=jax.ShapeDtypeStru...  30.8 us
    pallas_call x1, Pallas kernels, spectra(): pl.pallas_call(kernel, out_shape=out_shape, **call)  30.1 us

profile of v2, /device:TPU:9, one launch (start us, length us, event | category | flops | bytes accessed | tf_op | source)
XLA Modules:
  0.0 95.2 jit_solution(13522151672628142768)
XLA Ops:
  0.0 30.1 %forward_share.1.g_ref = f32[16,8,2,8,128]{4,3,2,1,0:T(8,128)} custom-call(bf16[32,8,256,256]{3,2,1,0:T(8,128)(2,1)} %f_ref.3, bf16[256,256]{1,0:T(8,128)(2,1)} %constant.22.clone.base_ref, bf16[128,256]{1,0:T(8,128)(2,1)} %constant.23.clone.y_ref), custom_call_target="tpu_custom_call" | custom-call | tf_op jit(solution)/shard_map/forward_share/pallas_call | solution.py:212
  30.1 30.8 %mix_share.1.q_ref = f32[16,2,8,8,128]{4,3,2,1,0:T(8,128)} custom-call(f32[16,8,2,8,128]{4,3,2,1,0:T(8,128)} %forward_share.1.g_ref, bf16[256,256]{1,0:T(8,128)(2,1)} %constant.24.clone.fhigh_ref, bf16[256,256]{1,0:T(8,128)(2,1)} %constant.25.clone.flow_ref, bf16[256,256]{1,0:T(8,128)(2,1)} %constant.26.clone.ihigh_ref, ...), custom_call_target="tpu_custom_call" | custom-call | tf_op jit(solution)/shard_map/mix_share/pallas_call | solution.py:312
  60.9 34.3 %inverse_planes.1 = bf16[32,8,256,256]{3,2,1,0:T(8,128)(2,1)} custom-call(bf16[32,8,256,256]{3,2,1,0:T(8,128)(2,1)} %f_ref.3, f32[16,2,8,8,128]{4,3,2,1,0:T(8,128)} %mix_share.1.q_ref, bf16[32,32]{1,0:T(8,128)(2,1)} %w_ref.3, bf16[256,32]{1,0:T(8,128)(2,1)} %constant.28.clone.left_ref, bf16[32,256]{1,0:T(8,128)(2,1)} %constant.29.clone.right_ref, ...), custom_call_target="tpu_custom_call" | custom-call | tf_op jit(solution)/shard_map/inverse_planes/pallas_call | solution.py:425

commit v3 on v2

--- a/solution.py
+++ b/solution.py
@@ -233,11 +233,11 @@
     return split(table.reshape(2 * QUAD * KX, 2 * length))
 
 
-def modes_kernel(g_ref, fhigh_ref, flow_ref, ihigh_ref, ilow_ref, w_ref, out_ref, *scratch):
+def modes_kernel(g_ref, fhigh_ref, flow_ref, ihigh_ref, ilow_ref, wreal_ref, wimag_ref, out_ref, *scratch):
     fhigh, flow, ihigh, ilow, turned, spectrum, blended, placed, sent, send, receive, local = scratch
     parts, planes, held_y, rows, _ = g_ref.shape
     length = parts * planes
-    channels = w_ref.shape[1]
+    channels = wreal_ref.shape[1]
     quads = KZ // QUAD
     groups = rows // 2
     here = pl.program_id(0)
@@ -248,7 +248,6 @@
         for q in range(QUAD):
             at = slice(q * 2 * length, (q + 1) * 2 * length)
             fhigh[at], flow[at] = chosen(fhigh_ref[...], 1, KX, QUAD, q), chosen(flow_ref[...], 1, KX, QUAD, q)
-            ihigh[:, at], ilow[:, at] = chosen(ihigh_ref[...], 0, KX, QUAD, q), chosen(ilow_ref[...], 0, KX, QUAD, q)
 
     for j in range(held_y):
 
@@ -270,11 +269,17 @@
         real, imag = total
         row = spectrum[here, pl.ds(i, 1), :]
         s_real, s_imag = row[:, :LANES], row[:, LANES:]
-        w_real, w_imag = w_ref[0, i], w_ref[1, i]
+        w_real, w_imag = wreal_ref[0, i], wimag_ref[0, i]
         return real + (s_real * w_real - s_imag * w_imag), imag + (s_real * w_imag + s_imag * w_real)
 
+    @pl.when(here == 1)
+    def widen():
+        for q in range(QUAD):
+            at = slice(q * 2 * length, (q + 1) * 2 * length)
+            ihigh[:, at], ilow[:, at] = chosen(ihigh_ref[...], 0, KX, QUAD, q), chosen(ilow_ref[...], 0, KX, QUAD, q)
+
     zero = jnp.zeros((channels, LANES), jnp.float32)
-    real, imag = lax.fori_loop(0, channels, mix, (zero, zero), unroll=4)
+    real, imag = lax.fori_loop(0, channels, mix, (zero, zero), unroll=8)
     blended[here, :, :LANES] = real
     blended[here, :, LANES:] = imag
 
@@ -315,7 +320,7 @@
         out_shape=jax.ShapeDtypeStruct(shape, jnp.float32),
         in_specs=[whole(*gathered.shape)]
         + [whole(*table.shape) for table in tables]
-        + [pl.BlockSpec((2, channels, channels, LANES), lambda b: (0, 0, 0, b))],
+        + [pl.BlockSpec((1, channels, channels, LANES), lambda b, part=part: (part, 0, 0, b)) for part in range(2)],
         out_specs=pl.BlockSpec(memory_space=pl.ANY),
         scratch_shapes=[pltpu.VMEM((wide, 2 * LANES), jnp.bfloat16)] * 2
         + [pltpu.VMEM((2 * LANES, wide), jnp.bfloat16)] * 2
@@ -329,7 +334,7 @@
         + [pltpu.SemaphoreType.DMA] * 3,
         compiler_params=pltpu.CompilerParams(vmem_limit_bytes=MOST, collective_id=1, has_side_effects=True),
         name="mix_share",
-    )(gathered, *map(jnp.asarray, tables), spectral_weight)
+    )(gathered, *map(jnp.asarray, tables), spectral_weight, spectral_weight)
 
 
 def inverse_kernel(f_ref, q_ref, w_ref, left_ref, right_ref, zhigh_ref, zlow_ref, y_ref, bias_ref, out_ref, *scratch):

time: 95.7 us -> 95.6 us (level)
  no operation moved by 1% of the time
where the time goes in v3:
time: 95.6 us; the launch traced here: 95.1 us
  Pallas kernels  95.1 us (99%)
    pallas_call x1, Pallas kernels, finish_planes(): pl.pallas_call(inverse_kernel, grid=(planes + 1,), out_shape=jax.ShapeDty...  34.3 us
    pallas_call x1, Pallas kernels, mix_on_device(): pl.pallas_call(modes_kernel, grid=(blocks,), out_shape=jax.ShapeDtypeStru...  30.7 us
    pallas_call x1, Pallas kernels, spectra(): pl.pallas_call(kernel, out_shape=out_shape, **call)  30.1 us

profile of v3, /device:TPU:9, one launch (start us, length us, event | category | flops | bytes accessed | tf_op | source)
XLA Modules:
  0.0 95.1 jit_solution(5305141033452267834)
XLA Ops:
  0.0 30.1 %forward_share.1.g_ref = f32[16,8,2,8,128]{4,3,2,1,0:T(8,128)} custom-call(bf16[32,8,256,256]{3,2,1,0:T(8,128)(2,1)} %f_ref.3, bf16[256,256]{1,0:T(8,128)(2,1)} %constant.22.clone.base_ref, bf16[128,256]{1,0:T(8,128)(2,1)} %constant.23.clone.y_ref), custom_call_target="tpu_custom_call" | custom-call | tf_op jit(solution)/shard_map/forward_share/pallas_call | solution.py:212
  30.1 30.7 %mix_share.1.q_ref = f32[16,2,8,8,128]{4,3,2,1,0:T(8,128)} custom-call(f32[16,8,2,8,128]{4,3,2,1,0:T(8,128)} %forward_share.1.g_ref, bf16[256,256]{1,0:T(8,128)(2,1)} %constant.24.clone.fhigh_ref, bf16[256,256]{1,0:T(8,128)(2,1)} %constant.25.clone.flow_ref, bf16[256,256]{1,0:T(8,128)(2,1)} %constant.26.clone.ihigh_ref, ...), custom_call_target="tpu_custom_call" | custom-call | tf_op jit(solution)/shard_map/mix_share/pallas_call | solution.py:317
  60.8 34.3 %inverse_planes.1 = bf16[32,8,256,256]{3,2,1,0:T(8,128)(2,1)} custom-call(bf16[32,8,256,256]{3,2,1,0:T(8,128)(2,1)} %f_ref.3, f32[16,2,8,8,128]{4,3,2,1,0:T(8,128)} %mix_share.1.q_ref, bf16[32,32]{1,0:T(8,128)(2,1)} %w_ref.1, bf16[256,32]{1,0:T(8,128)(2,1)} %constant.28.clone.left_ref, bf16[32,256]{1,0:T(8,128)(2,1)} %constant.29.clone.right_ref, ...), custom_call_target="tpu_custom_call" | custom-call | tf_op jit(solution)/shard_map/inverse_planes/pallas_call | solution.py:430
